TPU v7x, 256 devices: a whole 4x4x8 slice. The times are simulated.
256 devices in a mesh: seq: 8 (over y, x_lo), blk: 32 (over z, x_hi, core).
Axes of the slice: x: 4 (x_hi: 2, x_lo: 2; x = x_hi * 2 + x_lo), y: 4, z: 8, core: 2. Of those that a mesh axis runs over, the one named last changes fastest.
Arguments:
- activations: bfloat16 [2, 64, 1024, 4096], P(None, 'blk', 'seq'), may hold values from -120 to 120, as said below
- out_grads: bfloat16 [2, 64, 1024, 4096], P(None, 'blk', 'seq'), may hold values from -120 to 120, as said below
- lengths: int32 [64], P('blk'), may hold values from 512 to 1024
- input_proj: bfloat16 [2, 64, 4096], replicated, may hold values from -0.09375 to 0.09375
- output_proj: bfloat16 [2, 64, 4096], replicated, may hold values from -0.09375 to 0.09375
- stored_proj: float32 [16384, 2, 64, 64], P(('seq', 'blk')), may hold values from -6 to 6
Outputs:
- scores: float32 [64, 16384], P('blk', 'seq')
Inputs may be any that keep to these rules, and one draw needn't show every extreme that they name: `activations`: finite values. `out_grads`: finite values.
All inputs are finite; a program needn't handle non-finite values.
Results may differ from a plain program's by a relative error of at most 0.0003.
Values sent between devices are 32-bit elements; how exact they have to be, the bound alone decides.
No kernel may reach another device: no remote copies, remote signals or barrier semaphores. Data moves between devices by JAX's collectives and lax.ppermute only.
A program may use at most 64 MiB of HBM per device.

v0:
```python
import math
import jax
import jax.numpy as jnp
from jax import lax
from jax.sharding import PartitionSpec as P

damping = 0.1


def cut_along(x, dim, devices):
    before, after = (x.shape[:dim], x.shape[dim + 1 :])
    return jnp.moveaxis(x.reshape(*before, devices, -1, *after), dim, 0)


def sum_at_owner(x, axis, dim):
    pieces = cut_along(x, dim, lax.axis_size(axis))
    arrived = lax.all_to_all(pieces, axis, split_axis=0, concat_axis=0, tiled=True)
    return arrived.sum(axis=0)


def sent_together(arrays, axis, dim, along):
    columns = [a.reshape(*a.shape[:along], -1) for a in arrays]
    both = jnp.concatenate(columns, axis=along)
    whole, at, finished = (sum_at_owner(both, axis, dim), 0, [])
    for a, column in zip(arrays, columns):
        section = whole[..., at : at + column.shape[along]]
        finished.append(section.reshape(*section.shape[:along], *a.shape[along:]))
        at += column.shape[along]
    return tuple(finished)


def sent_to_all(x, axis):
    copies = jnp.broadcast_to(x, (lax.axis_size(axis), *x.shape))
    return lax.all_to_all(copies, axis, split_axis=0, concat_axis=0, tiled=True)


def of_everyone(x, axis):
    return sent_to_all(x, axis).sum(axis=0)


def together(arrays, axis):
    ravelled, at, finished = (jnp.concatenate([a.reshape(-1) for a in arrays]), 0, [])
    so_far = of_everyone(ravelled, axis)
    for a in arrays:
        finished.append(so_far[at : at + a.size].reshape(a.shape))
        at += a.size
    return tuple(finished)


def sent_together_2(arrays, axis, dim, along):
    widths = [a.shape[along] for a in arrays]
    both = jnp.concatenate(arrays, axis=along)
    whole = lax.all_gather(both, axis, axis=dim, tiled=True)
    return tuple(jnp.split(whole, [sum(widths[:k]) for k in range(1, len(widths))], axis=along))


def in_order(pieces, dim):
    shape = list(pieces.shape[1:])
    shape[dim] *= pieces.shape[0]
    return jnp.moveaxis(pieces, 0, dim).reshape(shape)


def gathered_copies(x, axis, dim):
    pieces = sent_to_all(x, axis)
    return in_order(pieces, dim)


def damped_inverse(moment, token_count):
    moment_mean = jnp.transpose(moment, (1, 0, 2)) / token_count
    proj_rank = moment_mean.shape[-1]
    identity = jnp.eye(proj_rank, dtype=jnp.float32)
    trace_part = jnp.trace(moment_mean, axis1=1, axis2=2)
    damped = moment_mean + (damping * trace_part / proj_rank)[:, None, None] * identity
    factor_low = jnp.linalg.cholesky(damped)
    return jax.vmap(lambda lower: jax.scipy.linalg.cho_solve((lower, True), identity))(factor_low)


def shards(activations, out_grads, lengths, input_proj, output_proj, stored_proj):
    hp = lax.Precision.HIGHEST
    layers, roll_dev, seq_dev, model_width = activations.shape
    proj_rank = input_proj.shape[1]
    seq_index = lax.axis_index("seq")
    blk_count = lax.axis_size("blk")
    train_dev = stored_proj.shape[0]
    positions = seq_index * seq_dev + jnp.arange(seq_dev, dtype=jnp.int32)
    live_mask = (positions[None, :] < lengths[:, None]).astype(jnp.float32)
    projected_in = (
        jnp.einsum("lrsd,lkd->lrsk", activations, input_proj, preferred_element_type=jnp.float32)
        * live_mask[None, :, :, None]
    )
    projected_out = (
        jnp.einsum("lrsd,lkd->lrsk", out_grads, output_proj, preferred_element_type=jnp.float32)
        * live_mask[None, :, :, None]
    )
    moment_in = jnp.einsum("lrsk,lrsm->klm", projected_in, projected_in, precision=hp)
    moment_out = jnp.einsum("lrsk,lrsm->klm", projected_out, projected_out, precision=hp)
    grad_terms = jnp.einsum("lrsp,lrsq->prlq", projected_out, projected_in, precision=hp)
    grad_rows, in_rows, out_rows = sent_together((grad_terms, moment_in, moment_out), "seq", 0, 2)
    local_count = jnp.sum(lengths).astype(jnp.float32)
    in_rows, out_rows, token_count = together((in_rows, out_rows, local_count), "blk")
    moment_in, moment_out = sent_together_2((in_rows, out_rows), "seq", 0, 1)
    factor_in = damped_inverse(moment_in, token_count)
    factor_out = damped_inverse(moment_out, token_count)
    right_done = jnp.einsum("prlq,lqk->prlk", grad_rows, factor_in, precision=hp)
    precond = jnp.zeros((proj_rank, roll_dev, layers, proj_rank), jnp.float32) + jnp.einsum(
        "lap,prlk->arlk", factor_out, gathered_copies(right_done, "seq", 0), precision=hp
    )
    norm_scale = 1.0 / math.sqrt(layers * proj_rank * proj_rank)
    empty_scores = jnp.zeros((roll_dev * blk_count, train_dev), jnp.float32)
    partial_scores = (
        jnp.einsum("prlk,tlpk->rt", gathered_copies(precond, "blk", 1), stored_proj, precision=hp)
        * norm_scale
    )
    local_scores = lax.dynamic_update_slice_in_dim(empty_scores, partial_scores, jnp.int32(0), 0)
    return lax.all_to_all(local_scores, "blk", split_axis=0, concat_axis=1, tiled=True)


def solution(mesh):
    return jax.shard_map(
        shards,
        mesh=mesh,
        in_specs=(
            P(None, "blk", "seq", None),
            P(None, "blk", "seq", None),
            P("blk"),
            P(),
            P(),
            P(("seq", "blk"), None, None, None),
        ),
        out_specs=P("blk", "seq"),
        check_vma=False,
    )
```

profile of v0, /device:TPU:1, one launch (start us, length us, event | category | flops | bytes accessed | tf_op | source)
XLA Modules:
  0.0 239.5 jit_solution(14124205600926753591)
XLA Ops:
  1.2 4.1 %convolution_multiply_fusion = f32[2,2,128,64]{2,3,1,0:T(8,128)S(1)} fusion(bf16[2,2,128,4096]{3,2,1,0:T(8,128)(2,1)} %param.10, bf16[2,64,4096]{2,1,0:T(8,128)(2,1)S(1)} %copy-done, f32[2,128]{1,0:T(2,128)S(1)} %compare_convert_fusion), kind=kOutput, calls=%fused_computation.2 | convolution fusion | flops 268468224 | bytes 5374976 | tf_op jit(solution)/shard_map/lrsd,lkd->lrsk/dot_general | solution.py:92
  5.7 1.4 convolution_multiply_fusion.1
  8.8 5.9 %all-to-all-start = ((f32[8,8,2,256]{3,1,2,0:T(8,128)}), f32[8,8,2,256]{3,1,2,0:T(8,128)S(1)}, u32[]{:S(2)}, u32[]{:S(2)}) async-start(f32[8,8,2,256]{3,1,2,0:T(8,128)} %copy.111), calls=%async_computation | async-start | bytes 262144 | tf_op jit(solution)/shard_map/all_to_all | solution.py:17
  16.1 4.3 %all-to-all-done = f32[8,8,2,256]{3,1,2,0:T(8,128)S(1)} async-done(((f32[8,8,2,256]{3,1,2,0:T(8,128)}), f32[8,8,2,256]{3,1,2,0:T(8,128)S(1)}, u32[]{:S(2)}, u32[]{:S(2)}) %all-to-all-start) | async-done | bytes 131104 | tf_op jit(solution)/shard_map/all_to_all | solution.py:17
  21.5 12.9 %all-to-all-start.1 = ((f32[32,1,2049]{2,1,0:T(1,128)}), f32[32,1,2049]{2,1,0:T(1,128)S(1)}, u32[]{:S(2)}, u32[]{:S(2)}) async-start(f32[32,1,2049]{2,1,0:T(1,128)} %broadcast_in_dim.37), calls=%async_computation.1 | async-start | bytes 557056 | tf_op jit(solution)/shard_map/all_to_all | solution.py:34
  34.6 13.0 %all-to-all-done.1 = f32[32,1,2049]{2,1,0:T(1,128)S(1)} async-done(((f32[32,1,2049]{2,1,0:T(1,128)}), f32[32,1,2049]{2,1,0:T(1,128)S(1)}, u32[]{:S(2)}, u32[]{:S(2)}) %all-to-all-start.1) | async-done | bytes 262304 | tf_op jit(solution)/shard_map/all_to_all | solution.py:34
  48.4 21.9 %all_gather.3 = f32[64,4,64]{2,1,0:T(4,128)S(1)} all-gather(f32[8,4,64]{2,1,0:T(4,128)S(1)} %pad_maximum_fusion.1), channel_id=1, replica_groups=mesh['seq'=8,'blk'=32] {'seq'}, dimensions={0}, use_global_device_ids=true | all-gather | bytes 73728 | tf_op jit(solution)/shard_map/all_gather | solution.py:53
  72.2 11.7 %custom-call.10 = f32[2,64,64]{2,1,0:T(8,128)S(1)} custom-call(f32[2,64,64]{2,1,0:T(8,128)S(1)} %fusion.14), custom_call_target="Cholesky" | custom-call | tf_op jit(solution)/shard_map/jit(cholesky)/cholesky | solution.py:74
  84.0 11.7 %custom-call.12 = f32[2,64,64]{2,1,0:T(8,128)S(1)} custom-call(f32[2,64,64]{2,1,0:T(8,128)S(1)} %fusion.9), custom_call_target="Cholesky" | custom-call | tf_op jit(solution)/shard_map/jit(cholesky)/cholesky | solution.py:74
  96.2 9.8 %custom-call.11 = f32[2,1,64,64]{2,3,1,0:T(8,128)S(1)} custom-call(f32[2,1,64,64]{3,2,1,0:T(8,128)S(1)} %get-tuple-element.19), custom_call_target="InvertDiagBlocksLowerTriangular" | custom-call | tf_op jit(solution)/shard_map/vmap(jit(_cho_solve))/triangular_solve | solution.py:75
  106.0 9.8 %custom-call.13 = f32[2,1,64,64]{2,3,1,0:T(8,128)S(1)} custom-call(f32[2,1,64,64]{3,2,1,0:T(8,128)S(1)} %get-tuple-element.20), custom_call_target="InvertDiagBlocksLowerTriangular" | custom-call | tf_op jit(solution)/shard_map/vmap(jit(_cho_solve))/triangular_solve | solution.py:75
  117.6 3.5 %all-to-all-start.2 = ((f32[8,1,2048]{2,1,0:T(1,128)}), f32[8,1,2048]{2,1,0:T(1,128)S(1)}, u32[]{:S(2)}, u32[]{:S(2)}) async-start(f32[8,1,2048]{2,1,0:T(1,128)} %reshape.116), calls=%async_computation.2 | async-start | bytes 131072 | tf_op jit(solution)/shard_map/all_to_all | solution.py:34
  121.3 4.7 %all-to-all-done.2 = f32[8,1,2048]{2,1,0:T(1,128)S(1)} async-done(((f32[8,1,2048]{2,1,0:T(1,128)}), f32[8,1,2048]{2,1,0:T(1,128)S(1)}, u32[]{:S(2)}, u32[]{:S(2)}) %all-to-all-start.2) | async-done | bytes 65568 | tf_op jit(solution)/shard_map/all_to_all | solution.py:34
  128.0 3.8 %broadcast_bitcast_fusion = f32[32,64,2,2,64]{4,3,2,1,0:T(2,128)} fusion(f32[64,2,2,64]{0,1,2,3:T(2,128)S(1)} %copy.127), kind=kLoop, calls=%fused_computation.59 | loop fusion | bytes 2162688
  131.8 6.6 %reshape.118 = f32[32,1,16384]{2,1,0:T(1,128)} reshape(f32[32,64,2,2,64]{4,3,2,1,0:T(2,128)} %broadcast_bitcast_fusion) | data formatting | bytes 4194304
  138.4 12.3 %all-to-all-start.3 = ((f32[32,1,16384]{2,1,0:T(1,128)}), f32[32,1,16384]{2,1,0:T(1,128)}, u32[]{:S(2)}, u32[]{:S(2)}) async-start(f32[32,1,16384]{2,1,0:T(1,128)} %reshape.118), calls=%async_computation.3 | async-start | bytes 4194304 | tf_op jit(solution)/shard_map/all_to_all | solution.py:34
  150.6 5.7 %copy.129 = f32[64,2,64,64]{2,0,1,3:T(8,128)} copy(f32[64,2,64,64]{3,2,1,0:T(8,128)} %param.14) | data formatting | bytes 4194304 | tf_op args[5]
  156.3 44.4 %all-to-all-done.3 = f32[32,1,16384]{2,1,0:T(1,128)} async-done(((f32[32,1,16384]{2,1,0:T(1,128)}), f32[32,1,16384]{2,1,0:T(1,128)}, u32[]{:S(2)}, u32[]{:S(2)}) %all-to-all-start.3) | async-done | bytes 2097184 | tf_op jit(solution)/shard_map/all_to_all | solution.py:34
  200.7 7.4 %reduce.6 = f32[32,16384]{1,0:T(8,128)S(1)} reduce(f32[32,1,16384]{2,1,0:T(1,128)} %all-to-all-done.3, f32[]{:T(128)} %broadcast.96), dimensions={1}, to_apply=%all_to_all.30.reduce_sub_computation | reduce | bytes 4194308 | tf_op jit(solution)/shard_map/all_to_all | solution.py:34
  208.1 4.4 %reshape.119 = f32[32,64,2,2,64]{4,3,2,1,0:T(2,128)} reshape(f32[32,16384]{1,0:T(8,128)S(1)} %reduce.6) | data formatting | bytes 4194304
  212.5 3.6 %bitcast_bitcast_fusion = f32[64,32,2,2,64]{0,2,3,4,1:T(2,128)S(1)} fusion(f32[32,64,2,2,64]{4,3,2,1,0:T(2,128)} %reshape.119), kind=kLoop, calls=%fused_computation.58 | loop fusion | bytes 4194304 | tf_op jit(solution)/shard_map/transpose | solution.py:60
  216.1 2.4 copy.128
  218.5 3.7 %fusion = f32[64,64]{1,0:T(8,128)S(1)} fusion(f32[64,64,2,64]{0,1,2,3:T(8,128)S(1)} %bitcast.112, f32[64,2,64,64]{2,0,1,3:T(8,128)S(1)} %copy-done.1), kind=kOutput, calls=%fused_computation.9 | convolution fusion | flops 402657280 | bytes 4210688 | tf_op jit(solution)/shard_map/prlk,tlpk->rt/dot_general | solution.py:111
  222.3 15.7 %all_to_all.40 = f32[32,1,128]{2,1,0:T(1,128)S(1)} all-to-all(f32[32,1,128]{2,1,0:T(1,128)S(1)} %reshape.120), channel_id=1, replica_groups=mesh['seq'=8,'blk'=32] {'blk'}, dimensions={0} | all-to-all | bytes 32768 | tf_op jit(solution)/shard_map/all_to_all | solution.py:115
  (74 shorter events, 13.7 us)
Async XLA Ops:
  0.0 1.2 copy-start
  0.0 5.7 %copy-start.3 = (bf16[2,64,4096]{2,1,0:T(8,128)(2,1)S(1)}, bf16[2,64,4096]{2,1,0:T(8,128)(2,1)}, u32[]{:S(2)}) copy-start(bf16[2,64,4096]{2,1,0:T(8,128)(2,1)} %param.12) | copy-start | bytes 3145732
  0.0 5.7 %copy-start.2 = (bf16[2,2,128,4096]{3,2,1,0:T(8,128)(2,1)S(1)}, bf16[2,2,128,4096]{3,2,1,0:T(8,128)(2,1)}, u32[]{:S(2)}) copy-start(bf16[2,2,128,4096]{3,2,1,0:T(8,128)(2,1)} %param.9) | copy-start | bytes 12582916
  5.4 9.4 %copy-start.4 = (s32[2]{0:T(128)S(1)}, s32[2]{0:T(128)}, u32[]{:S(2)}) copy-start(s32[2]{0:T(128)} %param.11) | copy-start | bytes 28
  8.8 11.5 %all-to-all-start = ((f32[8,8,2,256]{3,1,2,0:T(8,128)}), f32[8,8,2,256]{3,1,2,0:T(8,128)S(1)}, u32[]{:S(2)}, u32[]{:S(2)}) async-start(f32[8,8,2,256]{3,1,2,0:T(8,128)} %copy.111), calls=%async_computation | async-start | bytes 262144 | tf_op jit(solution)/shard_map/all_to_all | solution.py:17
  21.5 26.1 %all-to-all-start.1 = ((f32[32,1,2049]{2,1,0:T(1,128)}), f32[32,1,2049]{2,1,0:T(1,128)S(1)}, u32[]{:S(2)}, u32[]{:S(2)}) async-start(f32[32,1,2049]{2,1,0:T(1,128)} %broadcast_in_dim.37), calls=%async_computation.1 | async-start | bytes 557056 | tf_op jit(solution)/shard_map/all_to_all | solution.py:34
  117.6 8.5 %all-to-all-start.2 = ((f32[8,1,2048]{2,1,0:T(1,128)}), f32[8,1,2048]{2,1,0:T(1,128)S(1)}, u32[]{:S(2)}, u32[]{:S(2)}) async-start(f32[8,1,2048]{2,1,0:T(1,128)} %reshape.116), calls=%async_computation.2 | async-start | bytes 131072 | tf_op jit(solution)/shard_map/all_to_all | solution.py:34
  138.4 62.3 %all-to-all-start.3 = ((f32[32,1,16384]{2,1,0:T(1,128)}), f32[32,1,16384]{2,1,0:T(1,128)}, u32[]{:S(2)}, u32[]{:S(2)}) async-start(f32[32,1,16384]{2,1,0:T(1,128)} %reshape.118), calls=%async_computation.3 | async-start | bytes 4194304 | tf_op jit(solution)/shard_map/all_to_all | solution.py:34
  216.1 2.4 %copy-start.1 = (f32[64,2,64,64]{2,0,1,3:T(8,128)S(1)}, f32[64,2,64,64]{2,0,1,3:T(8,128)}, u32[]{:S(2)}) copy-start(f32[64,2,64,64]{2,0,1,3:T(8,128)} %copy.129) | copy-start | bytes 6291460
where the time goes:
time: 240 us; the launch traced here: 239 us
  waiting for transfers between devices  66.4 us (28%)
  other arithmetic  55.8 us (23%)
  blocking collectives  37.6 us (16%)
  starting transfers between devices  34.6 us (14%)
  local copies, waits for them, and re-layouts  32.5 us (14%)
  matrix products  11.6 us (5%)
    all_to_all x3, waiting for transfers between devices, sent_to_all(): return lax.all_to_all(copies, axis, split_axis=0, concat_axis=0, tiled=True)  62.1 us
    all_to_all x3, starting transfers between devices, sent_to_all(): return lax.all_to_all(copies, axis, split_axis=0, concat_axis=0, tiled=True)  28.6 us
    another operation x6, other arithmetic, damped_inverse(): factor_low = jnp.linalg.cholesky(damped)  23.7 us
    unnamed x21, local copies, waits for them, and re-layouts  22 us
    all_gather x1, blocking collectives, sent_together_2(): whole = lax.all_gather(both, axis, axis=dim, tiled=True)  21.9 us
    another operation x4, other arithmetic, damped_inverse(): jax.scipy.linalg.cho_solve((lower, True), identity)  19.8 us
    all_to_all x1, blocking collectives, shards(): lax.all_to_all(local_scores, 'blk', split_axis=0, concat_axis=1, tiled=True)  15.7 us
    all_to_all x2, other arithmetic, sent_to_all(): return lax.all_to_all(copies, axis, split_axis=0, concat_axis=0, tiled=True)  8.19 us
  transfers between devices with their start and end apart: 4, of which 4 were waited for; matrix products, arithmetic and copies ran while one was open for 3% of the time, Pallas kernels for 0%

commit v1 on v0

--- a/solution.py
+++ b/solution.py
@@ -5,6 +5,14 @@
 from jax.sharding import PartitionSpec as P
 
 damping = 0.1
+
+
+def refer_axis_part(block_here, chip_axis):
+    right_arr = lax.axis_size(chip_axis)
+    val = jnp.split(block_here, right_arr, axis=0)
+    part_now = jnp.stack(val)
+    r2 = lax.all_to_all(part_now, axis_name=chip_axis, split_axis=0, concat_axis=0)
+    return jnp.concatenate(r2, axis=1)
 
 
 def cut_along(x, dim, devices):
@@ -112,7 +120,7 @@
         * norm_scale
     )
     local_scores = lax.dynamic_update_slice_in_dim(empty_scores, partial_scores, jnp.int32(0), 0)
-    return lax.all_to_all(local_scores, "blk", split_axis=0, concat_axis=1, tiled=True)
+    return refer_axis_part(local_scores, "blk")
 
 
 def solution(mesh):

time: 240 us -> 241 us (level)
    unnamed x21 -> x52, local copies, waits for them, and re-layouts: 22 us -> 22.4 us
where the time goes in v1:
time: 241 us; the launch traced here: 240 us
  waiting for transfers between devices  66.4 us (28%)
  other arithmetic  55.8 us (23%)
  blocking collectives  37.6 us (16%)
  starting transfers between devices  34.6 us (14%)
  local copies, waits for them, and re-layouts  32.9 us (14%)
  matrix products  11.6 us (5%)
    all_to_all x3, waiting for transfers between devices, sent_to_all(): return lax.all_to_all(copies, axis, split_axis=0, concat_axis=0, tiled=True)  62.1 us
    all_to_all x3, starting transfers between devices, sent_to_all(): return lax.all_to_all(copies, axis, split_axis=0, concat_axis=0, tiled=True)  28.6 us
    another operation x6, other arithmetic, damped_inverse(): factor_low = jnp.linalg.cholesky(damped)  23.7 us
    unnamed x52, local copies, waits for them, and re-layouts  22.4 us
    all_gather x1, blocking collectives, sent_together_2(): whole = lax.all_gather(both, axis, axis=dim, tiled=True)  21.9 us
    another operation x4, other arithmetic, damped_inverse(): jax.scipy.linalg.cho_solve((lower, True), identity)  19.8 us
    all_to_all x1, blocking collectives, refer_axis_part(): lax.all_to_all(part_now, axis_name=chip_axis, split_axis=0, concat_axis=0)  15.7 us
    all_to_all x2, other arithmetic, sent_to_all(): return lax.all_to_all(copies, axis, split_axis=0, concat_axis=0, tiled=True)  8.19 us
  transfers between devices with their start and end apart: 4, of which 4 were waited for; matrix products, arithmetic and copies ran while one was open for 3% of the time, Pallas kernels for 0%

profile of v1, /device:TPU:1, one launch (start us, length us, event | category | flops | bytes accessed | tf_op | source)
XLA Modules:
  0.0 239.9 jit_solution(16061646483151694435)
XLA Ops:
  1.2 4.1 %convolution_multiply_fusion = f32[2,2,128,64]{2,3,1,0:T(8,128)S(1)} fusion(bf16[2,2,128,4096]{3,2,1,0:T(8,128)(2,1)} %param.10, bf16[2,64,4096]{2,1,0:T(8,128)(2,1)S(1)} %copy-done, f32[2,128]{1,0:T(2,128)S(1)} %compare_convert_fusion), kind=kOutput, calls=%fused_computation.2 | convolution fusion | flops 268468224 | bytes 5374976 | tf_op jit(solution)/shard_map/lrsd,lkd->lrsk/dot_general | solution.py:100
  5.7 1.4 convolution_multiply_fusion.1
  8.8 5.9 %all-to-all-start = ((f32[8,8,2,256]{3,1,2,0:T(8,128)}), f32[8,8,2,256]{3,1,2,0:T(8,128)S(1)}, u32[]{:S(2)}, u32[]{:S(2)}) async-start(f32[8,8,2,256]{3,1,2,0:T(8,128)} %copy.110), calls=%async_computation | async-start | bytes 262144 | tf_op jit(solution)/shard_map/all_to_all | solution.py:25
  16.1 4.3 %all-to-all-done = f32[8,8,2,256]{3,1,2,0:T(8,128)S(1)} async-done(((f32[8,8,2,256]{3,1,2,0:T(8,128)}), f32[8,8,2,256]{3,1,2,0:T(8,128)S(1)}, u32[]{:S(2)}, u32[]{:S(2)}) %all-to-all-start) | async-done | bytes 131104 | tf_op jit(solution)/shard_map/all_to_all | solution.py:25
  21.5 12.9 %all-to-all-start.1 = ((f32[32,1,2049]{2,1,0:T(1,128)}), f32[32,1,2049]{2,1,0:T(1,128)S(1)}, u32[]{:S(2)}, u32[]{:S(2)}) async-start(f32[32,1,2049]{2,1,0:T(1,128)} %broadcast_in_dim.37), calls=%async_computation.1 | async-start | bytes 557056 | tf_op jit(solution)/shard_map/all_to_all | solution.py:42
  34.6 13.0 %all-to-all-done.1 = f32[32,1,2049]{2,1,0:T(1,128)S(1)} async-done(((f32[32,1,2049]{2,1,0:T(1,128)}), f32[32,1,2049]{2,1,0:T(1,128)S(1)}, u32[]{:S(2)}, u32[]{:S(2)}) %all-to-all-start.1) | async-done | bytes 262304 | tf_op jit(solution)/shard_map/all_to_all | solution.py:42
  48.4 21.9 %all_gather.3 = f32[64,4,64]{2,1,0:T(4,128)S(1)} all-gather(f32[8,4,64]{2,1,0:T(4,128)S(1)} %pad_maximum_fusion.1), channel_id=1, replica_groups=mesh['seq'=8,'blk'=32] {'seq'}, dimensions={0}, use_global_device_ids=true | all-gather | bytes 73728 | tf_op jit(solution)/shard_map/all_gather | solution.py:61
  72.2 11.7 %custom-call.10 = f32[2,64,64]{2,1,0:T(8,128)S(1)} custom-call(f32[2,64,64]{2,1,0:T(8,128)S(1)} %fusion.14), custom_call_target="Cholesky" | custom-call | tf_op jit(solution)/shard_map/jit(cholesky)/cholesky | solution.py:82
  84.0 11.7 %custom-call.12 = f32[2,64,64]{2,1,0:T(8,128)S(1)} custom-call(f32[2,64,64]{2,1,0:T(8,128)S(1)} %fusion.9), custom_call_target="Cholesky" | custom-call | tf_op jit(solution)/shard_map/jit(cholesky)/cholesky | solution.py:82
  96.2 9.8 %custom-call.11 = f32[2,1,64,64]{2,3,1,0:T(8,128)S(1)} custom-call(f32[2,1,64,64]{3,2,1,0:T(8,128)S(1)} %get-tuple-element.19), custom_call_target="InvertDiagBlocksLowerTriangular" | custom-call | tf_op jit(solution)/shard_map/vmap(jit(_cho_solve))/triangular_solve | solution.py:83
  106.0 9.8 %custom-call.13 = f32[2,1,64,64]{2,3,1,0:T(8,128)S(1)} custom-call(f32[2,1,64,64]{3,2,1,0:T(8,128)S(1)} %get-tuple-element.20), custom_call_target="InvertDiagBlocksLowerTriangular" | custom-call | tf_op jit(solution)/shard_map/vmap(jit(_cho_solve))/triangular_solve | solution.py:83
  117.6 3.5 %all-to-all-start.2 = ((f32[8,1,2048]{2,1,0:T(1,128)}), f32[8,1,2048]{2,1,0:T(1,128)S(1)}, u32[]{:S(2)}, u32[]{:S(2)}) async-start(f32[8,1,2048]{2,1,0:T(1,128)} %reshape.121), calls=%async_computation.2 | async-start | bytes 131072 | tf_op jit(solution)/shard_map/all_to_all | solution.py:42
  121.3 4.7 %all-to-all-done.2 = f32[8,1,2048]{2,1,0:T(1,128)S(1)} async-done(((f32[8,1,2048]{2,1,0:T(1,128)}), f32[8,1,2048]{2,1,0:T(1,128)S(1)}, u32[]{:S(2)}, u32[]{:S(2)}) %all-to-all-start.2) | async-done | bytes 65568 | tf_op jit(solution)/shard_map/all_to_all | solution.py:42
  128.0 3.8 %broadcast_bitcast_fusion = f32[32,64,2,2,64]{4,3,2,1,0:T(2,128)} fusion(f32[64,2,2,64]{0,1,2,3:T(2,128)S(1)} %copy.126), kind=kLoop, calls=%fused_computation.123 | loop fusion | bytes 2162688
  131.8 6.6 %reshape.123 = f32[32,1,16384]{2,1,0:T(1,128)} reshape(f32[32,64,2,2,64]{4,3,2,1,0:T(2,128)} %broadcast_bitcast_fusion) | data formatting | bytes 4194304
  138.4 12.3 %all-to-all-start.3 = ((f32[32,1,16384]{2,1,0:T(1,128)}), f32[32,1,16384]{2,1,0:T(1,128)}, u32[]{:S(2)}, u32[]{:S(2)}) async-start(f32[32,1,16384]{2,1,0:T(1,128)} %reshape.123), calls=%async_computation.3 | async-start | bytes 4194304 | tf_op jit(solution)/shard_map/all_to_all | solution.py:42
  150.6 5.7 %copy.128 = f32[64,2,64,64]{2,0,1,3:T(8,128)} copy(f32[64,2,64,64]{3,2,1,0:T(8,128)} %param.14) | data formatting | bytes 4194304 | tf_op args[5]
  156.3 44.4 %all-to-all-done.3 = f32[32,1,16384]{2,1,0:T(1,128)} async-done(((f32[32,1,16384]{2,1,0:T(1,128)}), f32[32,1,16384]{2,1,0:T(1,128)}, u32[]{:S(2)}, u32[]{:S(2)}) %all-to-all-start.3) | async-done | bytes 2097184 | tf_op jit(solution)/shard_map/all_to_all | solution.py:42
  200.7 7.4 %reduce.6 = f32[32,16384]{1,0:T(8,128)S(1)} reduce(f32[32,1,16384]{2,1,0:T(1,128)} %all-to-all-done.3, f32[]{:T(128)} %broadcast.96), dimensions={1}, to_apply=%all_to_all.19.reduce_sub_computation | reduce | bytes 4194308 | tf_op jit(solution)/shard_map/all_to_all | solution.py:42
  208.1 4.4 %reshape.124 = f32[32,64,2,2,64]{4,3,2,1,0:T(2,128)} reshape(f32[32,16384]{1,0:T(8,128)S(1)} %reduce.6) | data formatting | bytes 4194304
  212.5 3.6 %bitcast_bitcast_fusion = f32[64,32,2,2,64]{0,2,3,4,1:T(2,128)S(1)} fusion(f32[32,64,2,2,64]{4,3,2,1,0:T(2,128)} %reshape.124), kind=kLoop, calls=%fused_computation.122 | loop fusion | bytes 4194304 | tf_op jit(solution)/shard_map/transpose | solution.py:68
  216.1 2.4 copy.127
  218.5 3.7 %fusion = f32[64,64]{1,0:T(8,128)S(1)} fusion(f32[64,64,2,64]{0,1,2,3:T(8,128)S(1)} %bitcast.239, f32[64,2,64,64]{2,0,1,3:T(8,128)S(1)} %copy-done.1), kind=kOutput, calls=%fused_computation.9 | convolution fusion | flops 402657280 | bytes 4210688 | tf_op jit(solution)/shard_map/prlk,tlpk->rt/dot_general | solution.py:119
  222.7 15.7 %all_to_all.26 = f32[32,1,128]{2,1,0:T(1,128)S(1)} all-to-all(f32[32,1,128]{2,1,0:T(1,128)S(1)} %reshape.125), channel_id=1, replica_groups=mesh['seq'=8,'blk'=32] {'blk'}, dimensions={0} | all-to-all | bytes 32768 | tf_op jit(solution)/shard_map/all_to_all | solution.py:14
  (106 shorter events, 14.0 us)
Async XLA Ops:
  0.0 1.2 copy-start
  0.0 5.7 %copy-start.3 = (bf16[2,64,4096]{2,1,0:T(8,128)(2,1)S(1)}, bf16[2,64,4096]{2,1,0:T(8,128)(2,1)}, u32[]{:S(2)}) copy-start(bf16[2,64,4096]{2,1,0:T(8,128)(2,1)} %param.12) | copy-start | bytes 3145732
  0.0 5.7 %copy-start.2 = (bf16[2,2,128,4096]{3,2,1,0:T(8,128)(2,1)S(1)}, bf16[2,2,128,4096]{3,2,1,0:T(8,128)(2,1)}, u32[]{:S(2)}) copy-start(bf16[2,2,128,4096]{3,2,1,0:T(8,128)(2,1)} %param.9) | copy-start | bytes 12582916
  5.4 9.4 %copy-start.4 = (s32[2]{0:T(128)S(1)}, s32[2]{0:T(128)}, u32[]{:S(2)}) copy-start(s32[2]{0:T(128)} %param.11) | copy-start | bytes 28
  8.8 11.5 %all-to-all-start = ((f32[8,8,2,256]{3,1,2,0:T(8,128)}), f32[8,8,2,256]{3,1,2,0:T(8,128)S(1)}, u32[]{:S(2)}, u32[]{:S(2)}) async-start(f32[8,8,2,256]{3,1,2,0:T(8,128)} %copy.110), calls=%async_computation | async-start | bytes 262144 | tf_op jit(solution)/shard_map/all_to_all | solution.py:25
  21.5 26.1 %all-to-all-start.1 = ((f32[32,1,2049]{2,1,0:T(1,128)}), f32[32,1,2049]{2,1,0:T(1,128)S(1)}, u32[]{:S(2)}, u32[]{:S(2)}) async-start(f32[32,1,2049]{2,1,0:T(1,128)} %broadcast_in_dim.37), calls=%async_computation.1 | async-start | bytes 557056 | tf_op jit(solution)/shard_map/all_to_all | solution.py:42
  117.6 8.5 %all-to-all-start.2 = ((f32[8,1,2048]{2,1,0:T(1,128)}), f32[8,1,2048]{2,1,0:T(1,128)S(1)}, u32[]{:S(2)}, u32[]{:S(2)}) async-start(f32[8,1,2048]{2,1,0:T(1,128)} %reshape.121), calls=%async_computation.2 | async-start | bytes 131072 | tf_op jit(solution)/shard_map/all_to_all | solution.py:42
  138.4 62.3 %all-to-all-start.3 = ((f32[32,1,16384]{2,1,0:T(1,128)}), f32[32,1,16384]{2,1,0:T(1,128)}, u32[]{:S(2)}, u32[]{:S(2)}) async-start(f32[32,1,16384]{2,1,0:T(1,128)} %reshape.123), calls=%async_computation.3 | async-start | bytes 4194304 | tf_op jit(solution)/shard_map/all_to_all | solution.py:42
  216.1 2.4 copy-start.1
